TPU v7x, 32 devices: a whole 2x2x4 slice. The times are simulated.
32 devices in a mesh: ctx: 8 (over y, x, core), head: 4 (over z).
Axes of the slice: x: 2, y: 2, z: 4, core: 2. Of those that a mesh axis runs over, the one named last changes fastest.
Arguments:
- q_latent: bfloat16 [2048, 1536], P('ctx', 'head'), may hold values from -70 to 70
- kv_latent: bfloat16 [2048, 576], P('ctx', 'head'), may hold values from -6 to 6
- w_query: bfloat16 [1536, 12288], P(None, 'head'), may hold values from -0.15625 to 0.15625
- w_key: bfloat16 [512, 8192], P(None, 'head'), may hold values from -0.25 to 0.25
- w_value: bfloat16 [512, 8192], P(None, 'head'), may hold values from -0.25 to 0.25
- d_out: bfloat16 [2048, 8192], P('ctx', 'head'), may hold values from -6 to 6
Outputs:
- attn_out: bfloat16 [2048, 8192], P('ctx', 'head')
- grad_qlat: float32 [2048, 1536], P('ctx', 'head')
- grad_kvlat: float32 [2048, 576], P('ctx', 'head')
All inputs are finite; a program needn't handle non-finite values.
Results may differ from a plain program's by a relative error of at most 0.023.
The roundings to bfloat16 on the way count: a program that leaves them out, or rounds other values in their place, can miss the bound.
Values may be sent and summed in bfloat16 or wider, within the bound.
A program may use at most 128 MiB of HBM per device.

v0:
```python
import jax
import jax.numpy as jnp
from jax import lax
from jax.sharding import PartitionSpec as P

KVL = 512
ROPE = 64
NOPE = 128
VDIM = 128
HEAD_DEV = 16


def from_behind(array, axis, by):
    peers = lax.axis_size(axis)
    pairs = [(i, i + by) for i in range(peers) if 0 <= i + by < peers]
    return lax.ppermute(array, axis, pairs)


def on_device(q_latent, kv_latent, w_query, w_key, w_value, d_out):
    block_rows = q_latent.shape[0]
    per_dev = HEAD_DEV
    width = NOPE + ROPE
    softmax_scale = width ** (-0.5)
    queries = jnp.dot(
        lax.all_gather(q_latent, "head", axis=1, tiled=True),
        w_query,
        preferred_element_type=jnp.float32,
    )
    queries = queries.astype(jnp.bfloat16).reshape(block_rows, per_dev, width)
    latent = lax.all_gather(kv_latent, "head", axis=1, tiled=True)

    def expand(latent_rows):
        main_cols = latent_rows[:, :KVL]
        keys_nope = jnp.dot(main_cols, w_key, preferred_element_type=jnp.float32).astype(
            jnp.bfloat16
        )
        values = jnp.dot(main_cols, w_value, preferred_element_type=jnp.float32).astype(
            jnp.bfloat16
        )
        return (
            keys_nope.reshape(block_rows, per_dev, NOPE),
            latent_rows[:, KVL:],
            values.reshape(block_rows, per_dev, VDIM),
        )

    own_keys = expand(latent)
    previous = expand(from_behind(latent, "ctx", 1))
    keys_all = jnp.concatenate([previous[0], own_keys[0]], 0)
    rope_all = jnp.concatenate([previous[1], own_keys[1]], 0)
    values_all = jnp.concatenate([previous[2], own_keys[2]], 0)
    leading = lax.axis_index("ctx") == 0
    query_pos = jnp.arange(block_rows)[:, None]
    key_pos = jnp.arange(2 * block_rows)[None, :]
    visible = jnp.where(
        key_pos < block_rows, jnp.logical_not(leading), key_pos - block_rows <= query_pos
    )[None]
    query_nope = queries[..., :NOPE]
    query_rope = queries[..., NOPE:]
    scores = jnp.einsum("qhd,khd->hqk", query_nope, keys_all, preferred_element_type=jnp.float32)
    scores = (
        scores + jnp.einsum("qhr,kr->hqk", query_rope, rope_all, preferred_element_type=jnp.float32)
    ) * softmax_scale
    scores = jnp.where(visible, scores, jnp.float32(-1e30))
    maxima = jnp.max(scores, -1, keepdims=True)
    expons = jnp.where(visible, jnp.exp(scores - maxima), jnp.float32(0.0))
    probs = expons / jnp.sum(expons, -1, keepdims=True)
    probs_b = probs.astype(jnp.bfloat16)
    output = jnp.einsum(
        "hqk,khd->qhd", probs_b, values_all, preferred_element_type=jnp.float32
    ).astype(jnp.bfloat16)
    grad_out = d_out.reshape(block_rows, per_dev, VDIM)
    dprob = jnp.einsum("qhd,khd->hqk", grad_out, values_all, preferred_element_type=jnp.float32)
    row_dot = jnp.sum(grad_out.astype(jnp.float32) * output.astype(jnp.float32), -1).T[..., None]
    dscore = (probs * (dprob - row_dot) * softmax_scale).astype(jnp.bfloat16)
    grad_qnope = jnp.einsum("hqk,khd->qhd", dscore, keys_all, preferred_element_type=jnp.float32)
    grad_qrope = jnp.einsum("hqk,kr->qhr", dscore, rope_all, preferred_element_type=jnp.float32)
    grad_query = (
        jnp.concatenate([grad_qnope, grad_qrope], -1)
        .astype(jnp.bfloat16)
        .reshape(block_rows, per_dev * width)
    )
    grad_qpart = jnp.dot(grad_query, w_query.T, preferred_element_type=jnp.float32)
    grad_knope = jnp.einsum(
        "hqk,qhd->khd", dscore, query_nope, preferred_element_type=jnp.float32
    ).astype(jnp.bfloat16)
    grad_krope = jnp.einsum(
        "hqk,qhr->khr", dscore, query_rope, preferred_element_type=jnp.float32
    ).astype(jnp.bfloat16)
    grad_value = jnp.einsum(
        "hqk,qhd->khd", probs_b, grad_out, preferred_element_type=jnp.float32
    ).astype(jnp.bfloat16)

    def project(knope_part, krope_part, value_part):
        main_cols = jnp.dot(
            knope_part.reshape(block_rows, per_dev * NOPE),
            w_key.T,
            preferred_element_type=jnp.float32,
        )
        main_cols = main_cols + jnp.dot(
            value_part.reshape(block_rows, per_dev * VDIM),
            w_value.T,
            preferred_element_type=jnp.float32,
        )
        rope_cols = jnp.sum(krope_part.astype(jnp.float32), axis=1)
        return jnp.concatenate([main_cols, rope_cols], -1)

    own_part = project(grad_knope[block_rows:], grad_krope[block_rows:], grad_value[block_rows:])
    earlier = project(grad_knope[:block_rows], grad_krope[:block_rows], grad_value[:block_rows])
    grad_kvpart = own_part + from_behind(earlier.astype(jnp.bfloat16), "ctx", -1).astype(
        earlier.dtype
    )
    grad_qlat, grad_kvlat = (
        lax.psum_scatter(grad_qpart, "head", scatter_dimension=1, tiled=True),
        lax.psum_scatter(grad_kvpart, "head", scatter_dimension=1, tiled=True),
    )
    return (output.reshape(block_rows, per_dev * VDIM), grad_qlat, grad_kvlat)


def solution(mesh):
    return jax.shard_map(
        on_device,
        mesh=mesh,
        in_specs=(
            P("ctx", "head"),
            P("ctx", "head"),
            P(None, "head"),
            P(None, "head"),
            P(None, "head"),
            P("ctx", "head"),
        ),
        out_specs=(P("ctx", "head"), P("ctx", "head"), P("ctx", "head")),
        check_vma=False,
    )
```

profile of v0, /device:TPU:0, one launch (start us, length us, event | category | flops | bytes accessed | tf_op | source)
XLA Modules:
  0.0 189.1 jit_solution(5349100622864666267)
XLA Ops:
  7.2 0.0 copy-start
  7.2 0.0 reduce-scatter.7.cloned.1.call-start
  7.2 16.0 %all_gather.6 = bf16[256,576]{0,1:T(8,128)(2,1)S(1)} all-gather(bf16[256,144]{0,1:T(8,128)(2,1)} %param.7), channel_id=1, replica_groups=mesh['ctx'=8,'head'=4] {'head'}, dimensions={1}, use_global_device_ids=true | all-gather | bytes 368640 | tf_op jit(solution)/shard_map/all_gather | solution.py:30
  23.2 2.0 %collective-permute-start = (bf16[256,576]{0,1:T(8,128)(2,1)S(1)}, bf16[256,576]{0,1:T(8,128)(2,1)}, u32[]{:S(2)}, u32[]{:S(2)}) collective-permute-start(bf16[256,576]{0,1:T(8,128)(2,1)S(1)} %all_gather.6), channel_id=1, source_target_pairs={{0,4},{4,8},{8,12},{12,16},{16,20},{20,24},{24,28},{1,5},{5,9},{9,... | collective-permute-start | bytes 884744 | tf_op jit(solution)/shard_map/ppermute | solution.py:16
  25.3 20.2 %all_gather.7 = bf16[256,1536]{1,0:T(8,128)(2,1)S(1)} all-gather(bf16[256,384]{1,0:T(8,128)(2,1)} %param.6), channel_id=1, replica_groups=mesh['ctx'=8,'head'=4] {'head'}, dimensions={1}, use_global_device_ids=true | all-gather | bytes 983040 | tf_op jit(solution)/shard_map/all_gather | solution.py:25
  45.5 3.3 %convolution_convert_fusion.3 = bf16[256,2048]{1,0:T(8,128)(2,1)} fusion(bf16[512,2048]{1,0:T(8,128)(2,1)} %param.10, bf16[256,576]{0,1:T(8,128)(2,1)S(1)} %all_gather.6), kind=kOutput, calls=%fused_computation.13 | convolution fusion | flops 537395200 | bytes 3407872 | tf_op jit(solution)/shard_map/dot_general | solution.py:37
  48.7 7.4 %convolution_convert_fusion = bf16[256,3072]{1,0:T(8,128)(2,1)} fusion(bf16[256,1536]{1,0:T(8,128)(2,1)S(1)} %all_gather.7, bf16[1536,3072]{1,0:T(8,128)(2,1)} %param.8), kind=kOutput, calls=%fused_computation.9 | convolution fusion | flops 2416705536 | bytes 11796480 | tf_op jit(solution)/shard_map/dot_general | solution.py:24
  56.1 0.7 fusion.15
  56.9 2.6 %copy.41 = bf16[256,3072]{0,1:T(8,128)(2,1)} copy(bf16[256,3072]{1,0:T(8,128)(2,1)} %convolution_convert_fusion) | data formatting | bytes 3145728 | tf_op jit(solution)/shard_map/convert_element_type | solution.py:29
  59.5 1.5 copy.46
  61.0 2.3 %copy.63 = bf16[256,2048]{0,1:T(8,128)(2,1)} copy(bf16[256,2048]{1,0:T(8,128)(2,1)} %convolution_convert_fusion.3) | data formatting | bytes 2097152 | tf_op jit(solution)/shard_map/reshape | solution.py:43
  63.3 0.0 copy-done
  63.3 1.7 fusion.7
  65.0 0.0 collective-permute-done
  65.0 0.0 copy-done.2
  65.0 2.7 %convolution_convert_fusion.4 = bf16[256,2048]{1,0:T(8,128)(2,1)} fusion(bf16[512,2048]{1,0:T(8,128)(2,1)S(1)} %copy-done.2, bf16[256,576]{0,1:T(8,128)(2,1)} %collective-permute-done), kind=kOutput, calls=%fused_computation.14 | convolution fusion | flops 537395200 | bytes 3407872 | tf_op jit(solution)/shard_map/dot_general | solution.py:37
  67.6 2.3 %copy.62 = bf16[256,2048]{0,1:T(8,128)(2,1)} copy(bf16[256,2048]{1,0:T(8,128)(2,1)} %convolution_convert_fusion.4) | data formatting | bytes 2097152 | tf_op jit(solution)/shard_map/reshape | solution.py:43
  69.9 1.8 fusion.6
  71.7 0.3 bitcast_dynamic-update-slice_fusion.1
  72.0 0.3 bitcast_dynamic-update-slice_fusion
  72.3 0.8 copy-done.6
  73.1 4.5 %fusion.12 = f32[16,256,512]{2,1,0:T(8,128)} fusion(bf16[512,16,128]{2,0,1:T(8,128)(2,1)S(1)} %bitcast_dynamic-update-slice_fusion, bf16[256,16,192]{0,2,1:T(8,128)(2,1)S(1)} %bitcast.82), kind=kOutput, calls=%fused_computation.35 | convolution fusion | flops 536870912 | bytes 11534336 | tf_op jit(solution)/shard_map/qhd,khd->hqk/dot_general | solution.py:59
  77.6 0.8 slice.51
  78.4 10.6 %fusion.28 = (f32[16,256]{1,0:T(8,128)S(1)}, f32[16,256,512]{2,1,0:T(8,128)}) fusion(pred[256,512]{1,0:T(8,128)(4,1)S(1)} %copy-done.14, f32[16,256,512]{2,1,0:T(8,128)} %fusion.12, bf16[256,16,192]{0,2,1:T(8,128)(2,1)} %bitcast.81, bf16[256,64]{0,1:T(8,128)(2,1)S(1)} %slice.52, bf16[256,64]{0,1:T(8,128)(2,1)S(1)} %slice.51), kind=kOutput, calls=%fused_computation.58 | convolution fusion | flops 281149952 | bytes 17645568 | tf_op jit(solution)/shard_map/sub | solution.py:65
  89.0 3.9 %fusion.5 = bf16[16,256,512]{2,1,0:T(8,128)(2,1)S(1)} fusion(f32[16,256,512]{2,1,0:T(8,128)} %get-tuple-element.17, f32[16,256]{1,0:T(8,128)S(1)} %get-tuple-element.16), kind=kLoop, calls=%fused_computation.10 | loop fusion | flops 4194304 | bytes 12599296 | tf_op jit(solution)/shard_map/convert_element_type | solution.py:67
  92.9 0.0 slice-start
  92.9 0.7 convert_bitcast_fusion
  93.7 0.5 copy-done.11
  94.1 0.3 copy-done.12
  94.5 2.5 %multiply_reduce_fusion = (f32[256,16]{0,1:T(8,128)S(1)}, bf16[16,128,256]{2,1,0:T(8,128)(2,1)}) fusion(bf16[256,2048]{0,1:T(8,128)(2,1)S(1)} %copy.46, bf16[16,256,512]{2,1,0:T(8,128)(2,1)S(1)} %fusion.5, bf16[256,16,128]{0,2,1:T(8,128)(2,1)S(1)} %bitcast.93, bf16[256,16,128]{0,2,1:T(8,128)(2,1)S(1)} %bitcast.95), kind=kOutput, calls=%fused_computation.18 | convolution fusion | flops 543682560 | bytes 8404992 | tf_op jit(solution)/shard_map/hqk,khd->qhd/dot_general | solution.py:68
  96.9 0.0 slice-done
  96.9 0.2 slice-done.1
  97.2 2.3 %fusion.2 = bf16[16,256,512]{2,1,0:T(8,128)(2,1)S(1)} fusion(f32[16,256]{1,0:T(8,128)S(1)} %bitcast.101, f32[16,256,512]{2,1,0:T(8,128)S(1)} %bitcast.86, f32[16,256]{1,0:T(8,128)S(1)} %get-tuple-element.16, bf16[256,16,128]{0,2,1:T(8,128)(2,1)S(1)} %bitcast.88, bf16[256,16,128]{0,2,1:T(8,128)(2,1)S(1)} %bitcast.94, bf16[256,16,128]{0,2,1:T(8,128)(2,1)S(1)} %bitcast.96), kind=kOutput, calls=%fused_computation.3 | convolution fusion | flops 551550976 | bytes 15761408 | tf_op jit(solution)/shard_map/qhd,khd->hqk/dot_general | solution.py:72
  99.5 0.0 copy-done.5
  99.5 0.0 copy-start.1
  99.5 1.5 fusion.8
  101.1 1.0 copy-done.7
  102.1 0.8 fusion.9
  103.0 0.7 convert_bitcast_fusion.1
  103.7 0.1 slice_reduce_fusion
  103.8 0.1 convert_reduce_fusion
  103.8 1.6 fusion.26
  105.4 0.3 fusion.27
  105.7 1.6 fusion.33
  107.3 1.6 fusion.32
  108.9 0.1 copy.53
  109.0 0.1 copy.52
  109.1 0.0 copy-start.3
  109.1 2.9 %fusion.11 = bf16[256,512]{1,0:T(8,128)(2,1)S(1)} fusion(f32[256,512]{1,0:T(8,128)} %fusion.33, bf16[256,2048]{0,1:T(8,128)(2,1)} %bitcast.97, bf16[512,2048]{1,0:T(8,128)(2,1)} %param.10), kind=kOutput, calls=%fused_computation.31 | convolution fusion | flops 537133056 | bytes 3932160 | tf_op jit(solution)/shard_map/dot_general | solution.py:99
  112.0 1.3 collective-permute-start.1
  113.4 0.8 convolution_add_fusion.1
  114.1 1.4 collective-permute-done.1
  115.6 0.9 maximum_add_fusion
  116.5 2.1 %copy.64 = f32[256,576]{0,1:T(8,128)} copy(f32[256,576]{1,0:T(8,128)} %maximum_add_fusion) | data formatting | bytes 1179648
  118.6 0.0 reduce-scatter.7.cloned.1.call-update
  118.6 0.0 reduce-scatter.5.cloned.1.call-start
  118.7 3.6 %fusion.10 = bf16[256,16,64]{0,2,1:T(8,128)(2,1)S(1)} fusion(bf16[16,256,512]{2,1,0:T(8,128)(2,1)} %copy-done.1, bf16[256,64]{0,1:T(8,128)(2,1)S(1)} %slice.52, bf16[256,64]{0,1:T(8,128)(2,1)S(1)} %slice.51), kind=kOutput, calls=%fused_computation.28 | convolution fusion | flops 268828672 | bytes 4784128 | tf_op jit(solution)/shard_map/hqk,kr->qhr/dot_general | solution.py:76
  122.3 0.1 pad_maximum_fusion.1
  122.4 7.6 %fusion.31 = f32[256,1536]{1,0:T(8,128)} fusion(bf16[256,3072]{0,1:T(8,128)(2,1)S(1)} %bitcast.91, bf16[1536,3072]{1,0:T(8,128)(2,1)} %param.8), kind=kOutput, calls=%fused_computation.59 | convolution fusion | flops 2415919104 | bytes 12582912 | tf_op jit(solution)/shard_map/dot_general | solution.py:82
  129.9 0.0 reduce-scatter.5.cloned.1.call-update
  130.0 1.2 copy-done.10
  131.2 1.4 copy.54
  132.6 13.0 %reduce-scatter.7.cloned.1.call-done = f32[144,256]{1,0:T(8,128)} async-done(((f32[576,256]{1,0:T(8,128)}), f32[144,256]{1,0:T(8,128)}) %reduce-scatter.7.cloned.1.call-update) | async-done | bytes 147472
  145.6 36.7 %reduce-scatter.5.cloned.1.call-done = f32[256,384]{1,0:T(8,128)} async-done(((f32[256,1536]{1,0:T(8,128)}), f32[256,384]{1,0:T(8,128)}) %reduce-scatter.5.cloned.1.call-update) | async-done | bytes 393232 | tf_op jit(solution)/shard_map/reduce_scatter | solution.py:113
  (25 shorter events, 0.1 us)
Async XLA Ops:
  7.2 56.1 %copy-start = (bf16[512,2048]{1,0:T(8,128)(2,1)S(1)}, bf16[512,2048]{1,0:T(8,128)(2,1)}, u32[]{:S(2)}) copy-start(bf16[512,2048]{1,0:T(8,128)(2,1)} %param.9) | copy-start | bytes 6291460
  7.2 138.4 %reduce-scatter.7.cloned.1.call-start = ((), (), s32[]{:S(2)}) async-start(), calls=%async_computation.3 | async-start | bytes 737280
  23.2 41.7 %collective-permute-start = (bf16[256,576]{0,1:T(8,128)(2,1)S(1)}, bf16[256,576]{0,1:T(8,128)(2,1)}, u32[]{:S(2)}, u32[]{:S(2)}) collective-permute-start(bf16[256,576]{0,1:T(8,128)(2,1)S(1)} %all_gather.6), channel_id=1, source_target_pairs={{0,4},{4,8},{8,12},{12,16},{16,20},{20,24},{24,28},{1,5},{5,9},{9,... | collective-permute-start | bytes 884744 | tf_op jit(solution)/shard_map/ppermute | solution.py:16
  63.3 1.7 copy-start.2
  69.9 2.1 %copy-start.8 = (bf16[32,16,8,128]{3,2,1,0:T(8,128)(2,1)S(1)}, bf16[32,16,8,128]{3,2,1,0:T(8,128)(2,1)}, u32[]{:S(2)}) copy-start(bf16[32,16,8,128]{3,2,1,0:T(8,128)(2,1)} %fusion.7) | copy-start | bytes 3145732
  71.7 1.4 copy-start.6
  72.3 5.3 %copy-start.4 = (bf16[512,16,128]{2,0,1:T(8,128)(2,1)}, bf16[512,16,128]{2,0,1:T(8,128)(2,1)S(1)}, u32[]{:S(2)}) copy-start(bf16[512,16,128]{2,0,1:T(8,128)(2,1)S(1)} %bitcast_dynamic-update-slice_fusion) | copy-start | bytes 6291460
  73.1 5.3 %copy-start.14 = (pred[256,512]{1,0:T(8,128)(4,1)S(1)}, pred[256,512]{1,0:T(8,128)(4,1)}, u32[]{:S(2)}) copy-start(pred[256,512]{1,0:T(8,128)(4,1)} %fusion.15) | copy-start | bytes 393220
  92.9 1.2 copy-start.11
  92.9 1.5 copy-start.12
  92.9 4.0 %slice-start = ((s8[8388608]{0:T(1024)(128)(4,1)}), s8[4194304]{0:T(1024)(128)(4,1)S(1)}, s32[]{:S(2)}) async-start(s8[8388608]{0:T(1024)(128)(4,1)} %bitcast.85), calls=%async_computation.4 | async-start | bytes 8388608
  94.5 2.7 %slice-start.1 = ((s8[8388608]{0:T(1024)(128)(4,1)}), s8[4194304]{0:T(1024)(128)(4,1)S(1)}, s32[]{:S(2)}) async-start(s8[8388608]{0:T(1024)(128)(4,1)} %bitcast.85), calls=%async_computation.5 | async-start | bytes 8388608
  97.2 2.3 %copy-start.5 = (bf16[512,16,128]{2,0,1:T(8,128)(2,1)S(1)}, bf16[512,16,128]{2,0,1:T(8,128)(2,1)}, u32[]{:S(2)}) copy-start(bf16[512,16,128]{2,0,1:T(8,128)(2,1)} %copy-done.4) | copy-start | bytes 6291460
  99.5 3.4 %copy-start.1 = (bf16[16,256,512]{2,1,0:T(8,128)(2,1)}, bf16[16,256,512]{2,1,0:T(8,128)(2,1)S(1)}, u32[]{:S(2)}) copy-start(bf16[16,256,512]{2,1,0:T(8,128)(2,1)S(1)} %fusion.2) | copy-start | bytes 12582916
  99.5 2.6 %copy-start.7 = (bf16[256,3072]{0,1:T(8,128)(2,1)S(1)}, bf16[256,3072]{0,1:T(8,128)(2,1)}, u32[]{:S(2)}) copy-start(bf16[256,3072]{0,1:T(8,128)(2,1)} %copy.41) | copy-start | bytes 4718596
  109.1 4.3 %copy-start.3 = (bf16[512,2048]{1,0:T(8,128)(2,1)S(1)}, bf16[512,2048]{1,0:T(8,128)(2,1)}, u32[]{:S(2)}) copy-start(bf16[512,2048]{1,0:T(8,128)(2,1)} %param.10) | copy-start | bytes 6291460
  109.1 4.3 %copy-start.9 = (bf16[256,16,128]{0,2,1:T(8,128)(2,1)S(1)}, bf16[256,16,128]{0,2,1:T(8,128)(2,1)}, u32[]{:S(2)}) copy-start(bf16[256,16,128]{0,2,1:T(8,128)(2,1)} %get-tuple-element.13) | copy-start | bytes 3145732
  109.1 4.3 %copy-start.13 = (f32[256,512]{1,0:T(8,128)S(1)}, f32[256,512]{1,0:T(8,128)}, u32[]{:S(2)}) copy-start(f32[256,512]{1,0:T(8,128)} %fusion.32) | copy-start | bytes 1572868
  112.0 3.5 %collective-permute-start.1 = (bf16[256,576]{1,0:T(8,128)(2,1)S(1)}, bf16[256,576]{1,0:T(8,128)(2,1)S(1)}, u32[]{:S(2)}, u32[]{:S(2)}) collective-permute-start(bf16[256,576]{1,0:T(8,128)(2,1)S(1)} %pad_maximum_fusion.4), channel_id=1, source_target_pairs={{4,0},{8,4},{12,8},{16,12},{20,16},{24,20},{28,24},{5,1},{9,5},{13... | collective-permute-start | bytes 884744 | tf_op jit(solution)/shard_map/ppermute | solution.py:16
  118.6 63.6 %reduce-scatter.5.cloned.1.call-start = ((), (), s32[]{:S(2)}) async-start(), calls=%async_computation.2 | async-start | bytes 1966080 | tf_op jit(solution)/shard_map/reduce_scatter | solution.py:113
  129.9 1.2 copy-start.10
Sparse Core Ops, SparseCore 0:
  118.8 26.7 reduce-scatter.6
  148.4 33.7 reduce-scatter.4
where the time goes:
time: 190 us; the launch traced here: 189 us
  matrix products  58.5 us (31%)
  waiting for transfers between devices  51.1 us (27%)
  blocking collectives  36.2 us (19%)
  local copies, waits for them, and re-layouts  19.7 us (10%)
  between operations  14.3 us (8%)
  other arithmetic  5.84 us (3%)
  starting transfers between devices  3.38 us (2%)
    reduce_scatter x1, waiting for transfers between devices, on_device(): lax.psum_scatter(grad_qpart, 'head', scatter_dimension=1, tiled=True)  36.7 us
    all_gather x1, blocking collectives, on_device(): lax.all_gather(q_latent, 'head', axis=1, tiled=True)  20.2 us
    all_gather x1, blocking collectives, on_device(): latent = lax.all_gather(kv_latent, 'head', axis=1, tiled=True)  16 us
    unnamed x3, waiting for transfers between devices  13 us
    sub x1, matrix products, on_device(): expons = jnp.where(visible, jnp.exp(scores - maxima), jnp.float32(0.0))  10.6 us
    unnamed x38, local copies, waits for them, and re-layouts  9.38 us
    dot_general x1, matrix products, on_device(): jnp.dot(grad_query, w_query.T, preferred_element_type=jnp.float32)  7.55 us
    dot_general x1, matrix products, on_device(): jnp.dot(lax.all_gather(q_latent, 'head', axis=1, tiled=True), w_query, pr...  7.4 us
  transfers between devices with their start and end apart: 4, of which 3 were waited for; matrix products, arithmetic and copies ran while one was open for 17% of the time, Pallas kernels for 0%

commit v1 on v0

--- a/solution.py
+++ b/solution.py
@@ -8,6 +8,13 @@
 NOPE = 128
 VDIM = 128
 HEAD_DEV = 16
+
+
+def swapped_in(x, mesh_axis, d):
+    size = lax.axis_size(mesh_axis)
+    parts = jnp.stack([x for _ in range(size)])
+    parts = lax.all_to_all(parts, mesh_axis, split_axis=0, concat_axis=0)
+    return jnp.concatenate(parts, axis=d)
 
 
 def from_behind(array, axis, by):
@@ -21,11 +28,7 @@
     per_dev = HEAD_DEV
     width = NOPE + ROPE
     softmax_scale = width ** (-0.5)
-    queries = jnp.dot(
-        lax.all_gather(q_latent, "head", axis=1, tiled=True),
-        w_query,
-        preferred_element_type=jnp.float32,
-    )
+    queries = jnp.dot(swapped_in(q_latent, "head", 1), w_query, preferred_element_type=jnp.float32)
     queries = queries.astype(jnp.bfloat16).reshape(block_rows, per_dev, width)
     latent = lax.all_gather(kv_latent, "head", axis=1, tiled=True)
 

time: 190 us -> 183 us (0.963)
  blocking collectives: 36.2 us -> 16 us
  starting transfers between devices: 3.38 us -> 8 us
  matrix products: 58.5 us -> 61.9 us
  waiting for transfers between devices: 51.1 us -> 54.4 us
  local copies, waits for them, and re-layouts: 19.7 us -> 21.9 us
    all_gather x1 -> x0, blocking collectives: 20.2 us -> none  [on_device(): lax.all_gather(q_latent, 'head', axis=1, tiled=True)]
    all_to_all x0 -> x1, starting transfers between devices: none -> 5.37 us  [swapped_in(): parts = lax.all_to_all(parts, mesh_axis, split_axis=0, concat_axis=0)]
    dot_general x1, matrix products: 1.51 us -> 4.64 us  [on_device(): jnp.einsum('hqk,khd->qhd', dscore, keys_all, preferred_element_type=jnp.f...]
    all_to_all x0 -> x1, waiting for transfers between devices: none -> 2.92 us  [swapped_in(): parts = lax.all_to_all(parts, mesh_axis, split_axis=0, concat_axis=0)]
    dot_general x1, matrix products: 4.54 us -> 6.48 us  [on_device(): jnp.einsum('qhd,khd->hqk', query_nope, keys_all, preferred_element_type=j...]
    unnamed x38 -> x35, local copies, waits for them, and re-layouts: 9.38 us -> 10.5 us
  transfers between devices with their start and end apart: 4 -> 5, of which waited for: 3 -> 4; matrix products, arithmetic and copies ran while one was open for 17% -> 18% of each run, Pallas kernels for 0% -> 0%
where the time goes in v1:
time: 183 us; the launch traced here: 182 us
  matrix products  61.9 us (34%)
  waiting for transfers between devices  54.4 us (30%)
  local copies, waits for them, and re-layouts  21.9 us (12%)
  blocking collectives  16 us (9%)
  between operations  14.3 us (8%)
  starting transfers between devices  8 us (4%)
  other arithmetic  5.92 us (3%)
    reduce_scatter x1, waiting for transfers between devices, on_device(): lax.psum_scatter(grad_qpart, 'head', scatter_dimension=1, tiled=True)  36.7 us
    all_gather x1, blocking collectives, on_device(): latent = lax.all_gather(kv_latent, 'head', axis=1, tiled=True)  16 us
    unnamed x3, waiting for transfers between devices  13.1 us
    sub x1, matrix products, on_device(): expons = jnp.where(visible, jnp.exp(scores - maxima), jnp.float32(0.0))  10.6 us
    unnamed x35, local copies, waits for them, and re-layouts  10.5 us
    dot_general x1, matrix products, on_device(): jnp.dot(grad_query, w_query.T, preferred_element_type=jnp.float32)  7.55 us
    dot_general x1, matrix products, on_device(): jnp.dot(swapped_in(q_latent, 'head', 1), w_query, preferred_element_type=...  7.47 us
    dot_general x1, matrix products, on_device(): jnp.einsum('qhd,khd->hqk', query_nope, keys_all, preferred_element_type=j...  6.48 us
  transfers between devices with their start and end apart: 5, of which 4 were waited for; matrix products, arithmetic and copies ran while one was open for 18% of the time, Pallas kernels for 0%

profile of v1, /device:TPU:0, one launch (start us, length us, event | category | flops | bytes accessed | tf_op | source)
XLA Modules:
  0.0 182.4 jit_solution(9700368672400016256)
XLA Ops:
  7.2 0.0 copy-start
  7.2 16.0 %all_gather.3 = bf16[256,576]{0,1:T(8,128)(2,1)S(1)} all-gather(bf16[256,144]{0,1:T(8,128)(2,1)} %param.7), channel_id=1, replica_groups=mesh['ctx'=8,'head'=4] {'head'}, dimensions={1}, use_global_device_ids=true | all-gather | bytes 368640 | tf_op jit(solution)/shard_map/all_gather | solution.py:33
  23.2 1.3 collective-permute-start
  24.5 1.1 copy.42
  25.6 1.0 stack.2
  26.6 5.4 %all-to-all-start = ((bf16[4,256,384]{1,2,0:T(8,128)(2,1)}), bf16[4,256,384]{1,2,0:T(8,128)(2,1)S(1)}, u32[]{:S(2)}, u32[]{:S(2)}) async-start(bf16[4,256,384]{1,2,0:T(8,128)(2,1)} %stack.2), calls=%async_computation | async-start | bytes 1572864 | tf_op jit(solution)/shard_map/all_to_all | solution.py:16
  31.9 0.0 reduce-scatter.7.cloned.1.call-start
  31.9 0.0 copy-start.2
  32.0 1.7 fusion.7
  33.7 1.7 convolution_convert_fusion.3
  35.4 0.8 fusion.15
  36.1 2.3 %copy.48 = bf16[256,2048]{0,1:T(8,128)(2,1)} copy(bf16[256,2048]{1,0:T(8,128)(2,1)} %param.11) | data formatting | bytes 2097152 | tf_op args[5]
  38.4 2.3 %copy.65 = bf16[256,2048]{0,1:T(8,128)(2,1)} copy(bf16[256,2048]{1,0:T(8,128)(2,1)} %convolution_convert_fusion.3) | data formatting | bytes 2097152 | tf_op jit(solution)/shard_map/reshape | solution.py:46
  40.7 0.0 collective-permute-done
  40.7 3.3 %convolution_convert_fusion.4 = bf16[256,2048]{1,0:T(8,128)(2,1)} fusion(bf16[512,2048]{1,0:T(8,128)(2,1)} %param.10, bf16[256,576]{0,1:T(8,128)(2,1)S(1)} %collective-permute-done), kind=kOutput, calls=%fused_computation.14 | convolution fusion | flops 537395200 | bytes 3407872 | tf_op jit(solution)/shard_map/dot_general | solution.py:40
  44.0 2.3 %copy.64 = bf16[256,2048]{0,1:T(8,128)(2,1)} copy(bf16[256,2048]{1,0:T(8,128)(2,1)} %convolution_convert_fusion.4) | data formatting | bytes 2097152 | tf_op jit(solution)/shard_map/reshape | solution.py:46
  46.3 0.7 fusion.6
  47.0 1.3 bitcast_dynamic-update-slice_fusion.1
  48.3 1.3 bitcast_dynamic-update-slice_fusion
  49.6 2.9 %all-to-all-done = bf16[4,256,384]{1,2,0:T(8,128)(2,1)S(1)} async-done(((bf16[4,256,384]{1,2,0:T(8,128)(2,1)}), bf16[4,256,384]{1,2,0:T(8,128)(2,1)S(1)}, u32[]{:S(2)}, u32[]{:S(2)}) %all-to-all-start) | async-done | bytes 786464 | tf_op jit(solution)/shard_map/all_to_all | solution.py:16
  52.5 7.5 %convolution_convert_fusion = bf16[256,3072]{1,0:T(8,128)(2,1)} fusion(bf16[256,1536]{0,1:T(8,128)(2,1)S(1)} %bitcast.90, bf16[1536,3072]{1,0:T(8,128)(2,1)} %param.8), kind=kOutput, calls=%fused_computation.9 | convolution fusion | flops 2416705536 | bytes 11796480 | tf_op jit(solution)/shard_map/dot_general | solution.py:31
  60.0 2.6 %copy.43 = bf16[256,3072]{0,1:T(8,128)(2,1)} copy(bf16[256,3072]{1,0:T(8,128)(2,1)} %convolution_convert_fusion) | data formatting | bytes 3145728 | tf_op jit(solution)/shard_map/convert_element_type | solution.py:32
  62.6 6.5 %fusion.12 = f32[16,256,512]{2,1,0:T(8,128)} fusion(bf16[512,16,128]{2,0,1:T(8,128)(2,1)} %bitcast_dynamic-update-slice_fusion, bf16[256,16,192]{0,2,1:T(8,128)(2,1)} %bitcast.84), kind=kOutput, calls=%fused_computation.35 | convolution fusion | flops 536870912 | bytes 11534336 | tf_op jit(solution)/shard_map/qhd,khd->hqk/dot_general | solution.py:62
  69.0 0.0 copy-done.12
  69.0 10.6 %fusion.28 = (f32[16,256]{1,0:T(8,128)S(1)}, f32[16,256,512]{2,1,0:T(8,128)}) fusion(pred[256,512]{1,0:T(8,128)(4,1)S(1)} %copy-done.12, f32[16,256,512]{2,1,0:T(8,128)} %fusion.12, bf16[256,16,192]{0,2,1:T(8,128)(2,1)} %bitcast.85, bf16[256,64]{0,1:T(8,128)(2,1)S(1)} %slice.52, bf16[256,64]{0,1:T(8,128)(2,1)S(1)} %slice.51), kind=kOutput, calls=%fused_computation.58 | convolution fusion | flops 281149952 | bytes 17645568 | tf_op jit(solution)/shard_map/sub | solution.py:68
  79.7 3.9 %fusion.5 = bf16[16,256,512]{2,1,0:T(8,128)(2,1)S(1)} fusion(f32[16,256,512]{2,1,0:T(8,128)} %get-tuple-element.17, f32[16,256]{1,0:T(8,128)S(1)} %get-tuple-element.16), kind=kLoop, calls=%fused_computation.10 | loop fusion | flops 4194304 | bytes 12599296 | tf_op jit(solution)/shard_map/convert_element_type | solution.py:70
  83.6 0.0 slice-start
  83.7 0.7 convert_bitcast_fusion
  84.4 0.5 copy-done.9
  84.9 0.3 copy-done.10
  85.2 2.5 %multiply_reduce_fusion = (f32[256,16]{0,1:T(8,128)S(1)}, bf16[16,128,256]{2,1,0:T(8,128)(2,1)}) fusion(bf16[256,2048]{0,1:T(8,128)(2,1)S(1)} %copy-done.5, bf16[16,256,512]{2,1,0:T(8,128)(2,1)S(1)} %fusion.5, bf16[256,16,128]{0,2,1:T(8,128)(2,1)S(1)} %bitcast.97, bf16[256,16,128]{0,2,1:T(8,128)(2,1)S(1)} %bitcast.99), kind=kOutput, calls=%fused_computation.18 | convolution fusion | flops 543682560 | bytes 8404992 | tf_op jit(solution)/shard_map/hqk,khd->qhd/dot_general | solution.py:71
  87.6 0.0 slice-done
  87.6 0.2 slice-done.1
  87.9 2.5 %fusion.2 = bf16[16,256,512]{2,1,0:T(8,128)(2,1)S(1)} fusion(f32[16,256]{1,0:T(8,128)S(1)} %bitcast.105, f32[16,256,512]{2,1,0:T(8,128)S(1)} %bitcast.89, f32[16,256]{1,0:T(8,128)S(1)} %get-tuple-element.16, bf16[256,16,128]{0,2,1:T(8,128)(2,1)S(1)} %bitcast.92, bf16[256,16,128]{0,2,1:T(8,128)(2,1)S(1)} %bitcast.98, bf16[256,16,128]{0,2,1:T(8,128)(2,1)S(1)} %bitcast.100), kind=kOutput, calls=%fused_computation.3 | convolution fusion | flops 551550976 | bytes 15761408 | tf_op jit(solution)/shard_map/qhd,khd->hqk/dot_general | solution.py:75
  90.4 4.6 %fusion.8 = bf16[256,16,128]{0,2,1:T(8,128)(2,1)S(1)} fusion(bf16[512,16,128]{2,0,1:T(8,128)(2,1)} %bitcast_dynamic-update-slice_fusion, bf16[16,256,512]{2,1,0:T(8,128)(2,1)S(1)} %fusion.2), kind=kOutput, calls=%fused_computation.25 | convolution fusion | flops 537395200 | bytes 7340032 | tf_op jit(solution)/shard_map/hqk,khd->qhd/dot_general | solution.py:78
  95.1 0.8 fusion.9
  95.9 0.7 convert_bitcast_fusion.1
  96.7 0.1 slice_reduce_fusion
  96.8 0.1 convert_reduce_fusion
  96.8 1.6 fusion.26
  98.4 0.2 fusion.27
  98.7 1.6 fusion.33
  100.3 1.6 fusion.32
  101.9 0.1 copy.55
  102.0 0.1 copy.54
  102.1 0.0 copy-start.3
  102.1 2.9 %fusion.11 = bf16[256,512]{1,0:T(8,128)(2,1)S(1)} fusion(f32[256,512]{1,0:T(8,128)} %fusion.33, bf16[256,2048]{0,1:T(8,128)(2,1)} %bitcast.101, bf16[512,2048]{1,0:T(8,128)(2,1)} %param.10), kind=kOutput, calls=%fused_computation.31 | convolution fusion | flops 537133056 | bytes 3932160 | tf_op jit(solution)/shard_map/dot_general | solution.py:102
  105.0 1.3 collective-permute-start.1
  106.3 0.0 copy-done.3
  106.4 0.0 copy-done.7
  106.4 0.8 convolution_add_fusion.1
  107.1 1.7 collective-permute-done.1
  108.8 0.9 maximum_add_fusion
  109.8 2.1 %copy.66 = f32[256,576]{0,1:T(8,128)} copy(f32[256,576]{1,0:T(8,128)} %maximum_add_fusion) | data formatting | bytes 1179648
  111.9 0.0 reduce-scatter.7.cloned.1.call-update
  111.9 0.0 reduce-scatter.5.cloned.1.call-start
  112.0 3.6 %fusion.10 = bf16[256,16,64]{0,2,1:T(8,128)(2,1)S(1)} fusion(bf16[16,256,512]{2,1,0:T(8,128)(2,1)} %copy-done.1, bf16[256,64]{0,1:T(8,128)(2,1)S(1)} %slice.52, bf16[256,64]{0,1:T(8,128)(2,1)S(1)} %slice.51), kind=kOutput, calls=%fused_computation.28 | convolution fusion | flops 268828672 | bytes 4784128 | tf_op jit(solution)/shard_map/hqk,kr->qhr/dot_general | solution.py:79
  115.5 0.1 pad_maximum_fusion.1
  115.6 7.5 %fusion.31 = f32[256,1536]{1,0:T(8,128)} fusion(bf16[256,3072]{0,1:T(8,128)(2,1)S(1)} %bitcast.95, bf16[1536,3072]{1,0:T(8,128)(2,1)} %param.8), kind=kOutput, calls=%fused_computation.59 | convolution fusion | flops 2415919104 | bytes 12582912 | tf_op jit(solution)/shard_map/dot_general | solution.py:85
  123.2 0.0 reduce-scatter.5.cloned.1.call-update
  123.2 1.2 copy-done.8
  124.4 1.4 copy.56
  125.8 13.1 %reduce-scatter.7.cloned.1.call-done = f32[144,256]{1,0:T(8,128)} async-done(((f32[576,256]{1,0:T(8,128)}), f32[144,256]{1,0:T(8,128)}) %reduce-scatter.7.cloned.1.call-update) | async-done | bytes 147472
  138.9 36.7 %reduce-scatter.5.cloned.1.call-done = f32[256,384]{1,0:T(8,128)} async-done(((f32[256,1536]{1,0:T(8,128)}), f32[256,384]{1,0:T(8,128)}) %reduce-scatter.5.cloned.1.call-update) | async-done | bytes 393232 | tf_op jit(solution)/shard_map/reduce_scatter | solution.py:116
  (24 shorter events, 0.1 us)
Async XLA Ops:
  7.2 24.8 %copy-start = (bf16[512,2048]{1,0:T(8,128)(2,1)S(1)}, bf16[512,2048]{1,0:T(8,128)(2,1)}, u32[]{:S(2)}) copy-start(bf16[512,2048]{1,0:T(8,128)(2,1)} %param.9) | copy-start | bytes 6291460
  23.2 17.5 %collective-permute-start = (bf16[256,576]{0,1:T(8,128)(2,1)S(1)}, bf16[256,576]{0,1:T(8,128)(2,1)S(1)}, u32[]{:S(2)}, u32[]{:S(2)}) collective-permute-start(bf16[256,576]{0,1:T(8,128)(2,1)S(1)} %all_gather.3), channel_id=1, source_target_pairs={{0,4},{4,8},{8,12},{12,16},{16,20},{20,24},{24,28},{1,5},{5,9},{9,... | collective-permute-start | bytes 884744 | tf_op jit(solution)/shard_map/ppermute | solution.py:23
  26.6 25.9 %all-to-all-start = ((bf16[4,256,384]{1,2,0:T(8,128)(2,1)}), bf16[4,256,384]{1,2,0:T(8,128)(2,1)S(1)}, u32[]{:S(2)}, u32[]{:S(2)}) async-start(bf16[4,256,384]{1,2,0:T(8,128)(2,1)} %stack.2), calls=%async_computation | async-start | bytes 1572864 | tf_op jit(solution)/shard_map/all_to_all | solution.py:16
  31.9 107.0 %reduce-scatter.7.cloned.1.call-start = ((), (), s32[]{:S(2)}) async-start(), calls=%async_computation.4 | async-start | bytes 737280
  31.9 1.7 copy-start.2
  46.3 2.1 %copy-start.6 = (bf16[32,16,8,128]{3,2,1,0:T(8,128)(2,1)S(1)}, bf16[32,16,8,128]{3,2,1,0:T(8,128)(2,1)}, u32[]{:S(2)}) copy-start(bf16[32,16,8,128]{3,2,1,0:T(8,128)(2,1)} %fusion.7) | copy-start | bytes 3145732
  62.6 6.5 %copy-start.12 = (pred[256,512]{1,0:T(8,128)(4,1)S(1)}, pred[256,512]{1,0:T(8,128)(4,1)}, u32[]{:S(2)}) copy-start(pred[256,512]{1,0:T(8,128)(4,1)} %fusion.15) | copy-start | bytes 393220
  79.7 3.9 %copy-start.5 = (bf16[256,2048]{0,1:T(8,128)(2,1)S(1)}, bf16[256,2048]{0,1:T(8,128)(2,1)}, u32[]{:S(2)}) copy-start(bf16[256,2048]{0,1:T(8,128)(2,1)} %copy.48) | copy-start | bytes 3145732
  83.6 1.2 copy-start.9
  83.6 1.5 copy-start.10
  83.6 4.0 %slice-start = ((s8[8388608]{0:T(1024)(128)(4,1)}), s8[4194304]{0:T(1024)(128)(4,1)S(1)}, s32[]{:S(2)}) async-start(s8[8388608]{0:T(1024)(128)(4,1)} %bitcast.88), calls=%async_computation.5 | async-start | bytes 8388608
  85.2 2.7 %slice-start.1 = ((s8[8388608]{0:T(1024)(128)(4,1)}), s8[4194304]{0:T(1024)(128)(4,1)S(1)}, s32[]{:S(2)}) async-start(s8[8388608]{0:T(1024)(128)(4,1)} %bitcast.88), calls=%async_computation.6 | async-start | bytes 8388608
  90.4 5.5 %copy-start.1 = (bf16[16,256,512]{2,1,0:T(8,128)(2,1)}, bf16[16,256,512]{2,1,0:T(8,128)(2,1)S(1)}, u32[]{:S(2)}) copy-start(bf16[16,256,512]{2,1,0:T(8,128)(2,1)S(1)} %fusion.2) | copy-start | bytes 12582916
  90.4 4.7 %copy-start.4 = (bf16[256,3072]{0,1:T(8,128)(2,1)S(1)}, bf16[256,3072]{0,1:T(8,128)(2,1)}, u32[]{:S(2)}) copy-start(bf16[256,3072]{0,1:T(8,128)(2,1)} %copy.43) | copy-start | bytes 4718596
  102.1 4.3 %copy-start.3 = (bf16[512,2048]{1,0:T(8,128)(2,1)S(1)}, bf16[512,2048]{1,0:T(8,128)(2,1)}, u32[]{:S(2)}) copy-start(bf16[512,2048]{1,0:T(8,128)(2,1)} %param.10) | copy-start | bytes 6291460
  102.1 4.3 %copy-start.7 = (bf16[256,16,128]{0,2,1:T(8,128)(2,1)S(1)}, bf16[256,16,128]{0,2,1:T(8,128)(2,1)}, u32[]{:S(2)}) copy-start(bf16[256,16,128]{0,2,1:T(8,128)(2,1)} %get-tuple-element.13) | copy-start | bytes 3145732
  102.1 4.3 %copy-start.11 = (f32[256,512]{1,0:T(8,128)S(1)}, f32[256,512]{1,0:T(8,128)}, u32[]{:S(2)}) copy-start(f32[256,512]{1,0:T(8,128)} %fusion.32) | copy-start | bytes 1572868
  105.0 3.8 %collective-permute-start.1 = (bf16[256,576]{1,0:T(8,128)(2,1)S(1)}, bf16[256,576]{1,0:T(8,128)(2,1)S(1)}, u32[]{:S(2)}, u32[]{:S(2)}) collective-permute-start(bf16[256,576]{1,0:T(8,128)(2,1)S(1)} %pad_maximum_fusion.4), channel_id=1, source_target_pairs={{4,0},{8,4},{12,8},{16,12},{20,16},{24,20},{28,24},{5,1},{9,5},{13... | collective-permute-start | bytes 884744 | tf_op jit(solution)/shard_map/ppermute | solution.py:23
  111.9 63.6 %reduce-scatter.5.cloned.1.call-start = ((), (), s32[]{:S(2)}) async-start(), calls=%async_computation.3 | async-start | bytes 1966080 | tf_op jit(solution)/shard_map/reduce_scatter | solution.py:116
  123.2 1.2 copy-start.8
Sparse Core Ops, SparseCore 0:
  112.0 26.8 reduce-scatter.6
  141.8 33.7 reduce-scatter.4
